TPU v7x, 256 devices: a whole 4x4x8 slice. The times are simulated.
256 devices in a mesh: wide: 32 (over z, x), group: 8 (over y, core).
Axes of the slice: x: 4, y: 4, z: 8, core: 2. Of those that a mesh axis runs over, the one named last changes fastest.
Arguments:
- feat4: bfloat16 [256, 24, 24, 256], P(('wide', 'group')), may hold values from -100 to 100
- feat5: bfloat16 [256, 12, 12, 256], P(('wide', 'group')), may hold values from -100 to 100
- feat6: bfloat16 [256, 6, 6, 256], P(('wide', 'group')), may hold values from -100 to 100
- feat7: bfloat16 [256, 3, 3, 256], P(('wide', 'group')), may hold values from -100 to 100
- out_grad4: bfloat16 [256, 24, 24, 256], P(('wide', 'group')), may hold values from -6 to 6
- out_grad5: bfloat16 [256, 12, 12, 256], P(('wide', 'group')), may hold values from -6 to 6
- out_grad6: bfloat16 [256, 6, 6, 256], P(('wide', 'group')), may hold values from -6 to 6
- out_grad7: bfloat16 [256, 3, 3, 256], P(('wide', 'group')), may hold values from -6 to 6
- conv_weight: bfloat16 [3, 3, 256, 256], replicated, may hold values from -0.125 to 0.125
- bn_gain: float32 [4, 256], replicated, may hold values from 0.25 to 1.75
- bn_shift: float32 [4, 256], replicated, may hold values from -0.5 to 0.5
- heights: int32 [256], P(('wide', 'group')), may hold values from 168 to 384
- widths: int32 [256], P(('wide', 'group')), may hold values from 168 to 384
Outputs:
- out4: bfloat16 [256, 24, 24, 256], P(('wide', 'group'))
- out5: bfloat16 [256, 12, 12, 256], P(('wide', 'group'))
- out6: bfloat16 [256, 6, 6, 256], P(('wide', 'group'))
- out7: bfloat16 [256, 3, 3, 256], P(('wide', 'group'))
- d_feat4: bfloat16 [256, 24, 24, 256], P(('wide', 'group'))
- d_feat5: bfloat16 [256, 12, 12, 256], P(('wide', 'group'))
- d_feat6: bfloat16 [256, 6, 6, 256], P(('wide', 'group'))
- d_feat7: bfloat16 [256, 3, 3, 256], P(('wide', 'group'))
- d_weight: float32 [3, 3, 256, 256], replicated
- d_gain: float32 [4, 256], replicated
- d_shift: float32 [4, 256], replicated
Inputs may be any that keep to these rules, and one draw needn't show every extreme that they name: `heights`: pixel height of the valid part of each image. `widths`: pixel width of the valid part of each image.
All inputs are finite; a program needn't handle non-finite values.
Results may differ from a plain program's by a relative error of at most 0.0049.
Values sent between devices are 32-bit elements; how exact they have to be, the bound alone decides.
A program may use at most 64 MiB of HBM per device.

v0:
```python
import jax
import jax.numpy as jnp
from jax import lax
from jax.sharding import Mesh
from jax.sharding import PartitionSpec as P

WIDE_GROUP = ("wide_0", "wide_1", "group_0", "group_1")
WIDE = ("wide_0", "wide_1")
GROUP = ("group_0", "group_1")


EPSILON = 1e-05


def by_axis(value, axes):
    for axis in axes:
        value = lax.psum(value, axis)
    return value


def split_up(value, dim, peers):
    before, after = (value.shape[:dim], value.shape[dim + 1 :])
    return jnp.moveaxis(value.reshape(*before, peers, -1, *after), dim, 0)


def summed_on_arrival(value, axis, dim):
    pieces = split_up(value, dim, lax.axis_size(axis))
    arrived = lax.all_to_all(pieces, axis, split_axis=0, concat_axis=0, tiled=True)
    return arrived.sum(axis=0)


def sum_by_axis(value, axes, dim):
    far, near = axes
    own = summed_on_arrival(split_up(value, dim, lax.axis_size(far)), near, dim + 1)
    return jnp.sum(lax.all_to_all(own, far, 0, 0, tiled=True), axis=0)


def padded_to(lines, peers):
    spare = -len(lines) % peers
    return jnp.pad(lines, [(0, spare)] + [(0, 0)] * (lines.ndim - 1))


def from_everyone(value, axis):
    peers = lax.axis_size(axis)
    return lax.all_to_all(
        jnp.broadcast_to(value[None], (peers, *value.shape)), axis, 0, 0, tiled=True
    )


def laid_out(pieces, dim):
    shape = list(pieces.shape[1:])
    shape[dim] *= pieces.shape[0]
    return jnp.moveaxis(pieces, 0, dim).reshape(shape)


def gathered_by_axis(value, axes, dim):
    far, near = axes
    initial = from_everyone(value, far)
    pieces = jnp.swapaxes(from_everyone(initial, near), 0, 1)
    return laid_out(pieces.reshape(-1, *value.shape), dim)


def total_of(value, axes):
    lines = value.reshape(-1, value.shape[-1])
    own = sum_by_axis(padded_to(lines, lax.axis_size(axes[0]) * lax.axis_size(axes[1])), axes, 0)
    whole = gathered_by_axis(own, axes, 0)
    return whole[: len(lines)].reshape(value.shape)


def level_mask(heights, widths, stride, extent):
    row_limit = (heights[0] + stride - 1) // stride
    col_limit = (widths[0] + stride - 1) // stride
    row_place = lax.broadcasted_iota(jnp.int32, (extent, extent), 0)
    col_place = lax.broadcasted_iota(jnp.int32, (extent, extent), 1)
    inside = jnp.logical_and(row_place < row_limit, col_place < col_limit)
    return (inside.astype(jnp.float32), row_limit)


def conv_rows(padded, conv_weight, start_row, row_count, extent):
    summed = jnp.zeros((row_count * extent, conv_weight.shape[3]), jnp.float32)
    for tap_row in range(3):
        for tap_col in range(3):
            window = lax.dynamic_slice_in_dim(padded, start_row + tap_row, row_count, 0)[
                :, tap_col : tap_col + extent, :
            ]
            summed = summed + jnp.dot(
                window.reshape(row_count * extent, -1),
                conv_weight[tap_row, tap_col],
                preferred_element_type=jnp.float32,
            )
    return summed.reshape(row_count, extent, -1)


def input_grad_rows(padded_back, conv_weight, start_row, row_count, extent):
    summed = jnp.zeros((row_count * extent, conv_weight.shape[2]), jnp.float32)
    for tap_row in range(3):
        for tap_col in range(3):
            window = lax.dynamic_slice_in_dim(padded_back, start_row + 2 - tap_row, row_count, 0)[
                :, 2 - tap_col : 2 - tap_col + extent, :
            ]
            summed = summed + lax.dot_general(
                window.reshape(row_count * extent, -1),
                conv_weight[tap_row, tap_col],
                (((1,), (1,)), ((), ())),
                preferred_element_type=jnp.float32,
            )
    return summed.reshape(row_count, extent, -1)


def weight_grad_rows(padded, back_rows, start_row, row_count, extent):
    flat_back = back_rows.reshape(row_count * extent, -1)
    tap_terms = []
    for tap_row in range(3):
        for tap_col in range(3):
            window = lax.dynamic_slice_in_dim(padded, start_row + tap_row, row_count, 0)[
                :, tap_col : tap_col + extent, :
            ]
            tap_terms.append(
                lax.dot_general(
                    window.reshape(row_count * extent, -1),
                    flat_back,
                    (((0,), (0,)), ((), ())),
                    preferred_element_type=jnp.float32,
                )
            )
    return jnp.stack(tap_terms).reshape(3, 3, padded.shape[2], flat_back.shape[1])


def forward_conv(padded, conv_weight, extent):
    conv_out = conv_rows(padded, conv_weight, 0, extent, extent)
    return conv_out


def backward_conv(padded, back_grad, conv_weight, extent):
    padded_back = jnp.pad(back_grad, ((1, 1), (1, 1), (0, 0)))
    weight_part = weight_grad_rows(padded, back_grad, 0, extent, extent)
    input_part = input_grad_rows(padded_back, conv_weight, 0, extent, extent)
    return (weight_part, input_part)


def combine_stats(values):
    result = jax.tree.map(lambda part: by_axis(part, WIDE_GROUP), values)
    return result


def combine_grads(values):
    result = total_of(values, (("wide_0", "wide_1"), ("group_0", "group_1")))
    return result


def shards(
    feat4,
    feat5,
    feat6,
    feat7,
    out_grad4,
    out_grad5,
    out_grad6,
    out_grad7,
    conv_weight,
    bn_gain,
    bn_shift,
    heights,
    widths,
):
    features = (feat4, feat5, feat6, feat7)
    cotangents = (out_grad4, out_grad5, out_grad6, out_grad7)
    devices = lax.axis_size(WIDE) * lax.axis_size(GROUP)
    levels = []
    for level_index in range(4):
        feature = features[level_index][0]
        extent = feature.shape[0]
        valid_mask, row_limit = level_mask(heights, widths, 16 * 2**level_index, extent)
        weighted = valid_mask[:, :, None]
        padded = jnp.pad(feature * weighted.astype(feature.dtype), ((1, 1), (1, 1), (0, 0)))
        conv_out = forward_conv(padded, conv_weight, extent)
        levels.append((valid_mask, row_limit, weighted, padded, conv_out))
    moments = []
    local_sums = jnp.stack(
        [jnp.sum(level_entry[4] * level_entry[2], axis=(0, 1)) for level_entry in levels]
    )
    local_squares = jnp.stack(
        [
            jnp.sum(level_entry[2] * level_entry[4] * level_entry[4], axis=(0, 1))
            for level_entry in levels
        ]
    )
    local_counts = jnp.stack([jnp.sum(level_entry[0]) for level_entry in levels])
    moment_sums, squares, counts = combine_stats((local_sums, local_squares, local_counts))
    for level_index in range(4):
        pixel_count = counts[level_index]
        mean_value = moment_sums[level_index] / pixel_count
        moments.append(
            (pixel_count, mean_value, squares[level_index] / pixel_count - mean_value * mean_value)
        )
    finals = []
    for level_index in range(4):
        valid_mask, row_limit, weighted, padded, conv_out = levels[level_index]
        pixel_count, mean_value, variance = moments[level_index]
        inverse = lax.rsqrt(variance + EPSILON)
        normed = (conv_out - mean_value) * inverse
        shifted = bn_gain[level_index] * normed + bn_shift[level_index]
        sigmoid_value = jax.nn.sigmoid(shifted)
        output = (weighted * shifted * sigmoid_value).astype(jnp.bfloat16)
        slope_term = (
            weighted
            * cotangents[level_index][0].astype(jnp.float32)
            * sigmoid_value
            * (1.0 + shifted * (1.0 - sigmoid_value))
        )
        finals.append((output, normed, inverse, slope_term))
    shift_local = jnp.stack([jnp.sum(final_entry[3], axis=(0, 1)) for final_entry in finals])
    gain_local = jnp.stack(
        [jnp.sum(final_entry[3] * final_entry[1], axis=(0, 1)) for final_entry in finals]
    )
    shift_rows, gain_rows = combine_stats((shift_local, gain_local))
    back_sums = [(shift_rows[level_index], gain_rows[level_index]) for level_index in range(4)]
    weight_local = jnp.zeros(conv_weight.shape, jnp.float32)
    outputs = []
    input_grads = []
    shift_list = []
    gain_list = []
    for level_index in range(4):
        valid_mask, row_limit, weighted, padded, conv_out = levels[level_index]
        pixel_count, mean_value, variance = moments[level_index]
        output, normed, inverse, slope_term = finals[level_index]
        shift_sum, gain_sum = back_sums[level_index]
        extent = conv_out.shape[0]
        back_grad = (
            weighted
            * (bn_gain[level_index] * inverse)
            * (slope_term - shift_sum / pixel_count - normed * (gain_sum / pixel_count))
        ).astype(jnp.bfloat16)
        weight_part, input_part = backward_conv(padded, back_grad, conv_weight, extent)
        weight_local = weight_local + weight_part
        input_grads.append((weighted * input_part).astype(jnp.bfloat16)[None])
        outputs.append(output[None])
        shift_list.append(shift_sum)
        gain_list.append(gain_sum)
    weight_total = combine_grads(weight_local)
    return (
        outputs[0],
        outputs[1],
        outputs[2],
        outputs[3],
        input_grads[0],
        input_grads[1],
        input_grads[2],
        input_grads[3],
        weight_total / devices,
        jnp.stack(gain_list) / devices,
        jnp.stack(shift_list) / devices,
    )


def solution(mesh):
    torus = Mesh(mesh.devices.reshape(8, 4, 4, 2), ("wide_0", "wide_1", "group_0", "group_1"))
    in_specs = (
        P(WIDE_GROUP, None, None, None),
        P(WIDE_GROUP, None, None, None),
        P(WIDE_GROUP, None, None, None),
        P(WIDE_GROUP, None, None, None),
        P(WIDE_GROUP, None, None, None),
        P(WIDE_GROUP, None, None, None),
        P(WIDE_GROUP, None, None, None),
        P(WIDE_GROUP, None, None, None),
        P(),
        P(),
        P(),
        P(WIDE_GROUP),
        P(WIDE_GROUP),
    )
    out_specs = (
        P(WIDE_GROUP, None, None, None),
        P(WIDE_GROUP, None, None, None),
        P(WIDE_GROUP, None, None, None),
        P(WIDE_GROUP, None, None, None),
        P(WIDE_GROUP, None, None, None),
        P(WIDE_GROUP, None, None, None),
        P(WIDE_GROUP, None, None, None),
        P(WIDE_GROUP, None, None, None),
        P(),
        P(),
        P(),
    )
    return jax.shard_map(
        shards, mesh=torus, in_specs=in_specs, out_specs=out_specs, check_vma=False
    )
```

profile of v0, /device:TPU:1, one launch (start us, length us, event | category | flops | bytes accessed | tf_op | source)
XLA Modules:
  0.0 288.3 jit_solution(2735352045582360944)
XLA Ops:
  9.6 1.0 fusion.131
  10.7 1.1 convolution_add_fusion.63
  11.7 1.1 convolution_add_fusion.62
  27.2 2.6 pad_maximum_fusion.4
  29.8 17.7 %all-reduce.9 = (f32[4,256]{1,0:T(4,128)S(1)}, f32[4]{0:T(128)S(1)}, f32[4,256]{1,0:T(4,128)S(1)}) all-reduce(f32[4,256]{1,0:T(4,128)S(1)} %pad_maximum_fusion.1, f32[4]{0:T(128)S(1)} %pad_maximum_fusion.4, f32[4,256]{1,0:T(4,128)S(1)} %pad_maximum_fusion), channel_id=1, replica_groups=mesh['wide_0'=8,'wide_1'=4,'group_0'=4,'group_1'=2] {'wide_0'}, use_global_device_ids=true, to_apply=%region_20.21 | all-reduce | flops 2052 | bytes 16416 | tf_op jit(solution)/shard_map/psum | solution.py:17
  47.5 8.7 %all-reduce.13 = (f32[4,256]{1,0:T(4,128)S(1)}, f32[4]{0:T(128)S(1)}, f32[4,256]{1,0:T(4,128)S(1)}) all-reduce(f32[4,256]{1,0:T(4,128)S(1)} %get-tuple-element.29, f32[4]{0:T(128)S(1)} %get-tuple-element.30, f32[4,256]{1,0:T(4,128)S(1)} %get-tuple-element.31), channel_id=1, replica_groups=mesh['wide_0'=8,'wide_1'=4,'group_0'=4,'group_1'=2] {'wide_1'}, use_global_device_ids=true, to_apply=%region_21.22 | all-reduce | flops 2052 | bytes 16416 | tf_op jit(solution)/shard_map/psum | solution.py:17
  56.2 9.0 %all-reduce.11 = (f32[4,256]{1,0:T(4,128)S(1)}, f32[4]{0:T(128)S(1)}, f32[4,256]{1,0:T(4,128)S(1)}) all-reduce(f32[4,256]{1,0:T(4,128)S(1)} %get-tuple-element.39, f32[4]{0:T(128)S(1)} %get-tuple-element.40, f32[4,256]{1,0:T(4,128)S(1)} %get-tuple-element.41), channel_id=1, replica_groups=mesh['wide_0'=8,'wide_1'=4,'group_0'=4,'group_1'=2] {'group_0'}, use_global_device_ids=true, to_apply=%region_22.23 | all-reduce | flops 2052 | bytes 16416 | tf_op jit(solution)/shard_map/psum | solution.py:17
  65.2 10.5 %all-reduce.15 = (f32[4,256]{1,0:T(4,128)S(1)}, f32[4]{0:T(128)S(1)}, f32[4,256]{1,0:T(4,128)S(1)}) all-reduce(f32[4,256]{1,0:T(4,128)S(1)} %get-tuple-element.34, f32[4]{0:T(128)S(1)} %get-tuple-element.35, f32[4,256]{1,0:T(4,128)S(1)} %get-tuple-element.36), channel_id=1, replica_groups=mesh['wide_0'=8,'wide_1'=4,'group_0'=4,'group_1'=2] {'group_1'}, use_global_device_ids=true, to_apply=%region_23.24 | all-reduce | flops 2052 | bytes 16416 | tf_op jit(solution)/shard_map/psum | solution.py:17
  76.4 2.5 slice_divide_fusion.8
  78.9 2.5 slice_divide_fusion.9
  85.3 11.0 %all-reduce.8 = (f32[4,256]{1,0:T(4,128)S(1)}, f32[4,256]{1,0:T(4,128)S(1)}) all-reduce(f32[4,256]{1,0:T(4,128)S(1)} %pad_maximum_fusion.3, f32[4,256]{1,0:T(4,128)S(1)} %pad_maximum_fusion.2), channel_id=1, replica_groups=mesh['wide_0'=8,'wide_1'=4,'group_0'=4,'group_1'=2] {'wide_0'}, use_global_device_ids=true, to_apply=%region_36.37 | all-reduce | flops 2048 | bytes 16384 | tf_op jit(solution)/shard_map/psum | solution.py:17
  96.3 6.1 %all-reduce.12 = (f32[4,256]{1,0:T(4,128)S(1)}, f32[4,256]{1,0:T(4,128)S(1)}) all-reduce(f32[4,256]{1,0:T(4,128)S(1)} %get-tuple-element.27, f32[4,256]{1,0:T(4,128)S(1)} %get-tuple-element.28), channel_id=1, replica_groups=mesh['wide_0'=8,'wide_1'=4,'group_0'=4,'group_1'=2] {'wide_1'}, use_global_device_ids=true, to_apply=%region_37.38 | all-reduce | flops 2048 | bytes 16384 | tf_op jit(solution)/shard_map/psum | solution.py:17
  102.4 6.1 %all-reduce.10 = (f32[4,256]{1,0:T(4,128)S(1)}, f32[4,256]{1,0:T(4,128)S(1)}) all-reduce(f32[4,256]{1,0:T(4,128)S(1)} %get-tuple-element.37, f32[4,256]{1,0:T(4,128)S(1)} %get-tuple-element.38), channel_id=1, replica_groups=mesh['wide_0'=8,'wide_1'=4,'group_0'=4,'group_1'=2] {'group_0'}, use_global_device_ids=true, to_apply=%region_38.39 | all-reduce | flops 2048 | bytes 16384 | tf_op jit(solution)/shard_map/psum | solution.py:17
  108.5 9.4 %all-reduce.14 = (f32[4,256]{1,0:T(4,128)S(1)}, f32[4,256]{1,0:T(4,128)S(1)}) all-reduce(f32[4,256]{1,0:T(4,128)S(1)} %get-tuple-element.32, f32[4,256]{1,0:T(4,128)S(1)} %get-tuple-element.33), channel_id=1, replica_groups=mesh['wide_0'=8,'wide_1'=4,'group_0'=4,'group_1'=2] {'group_1'}, use_global_device_ids=true, to_apply=%region_39.40 | all-reduce | flops 2048 | bytes 16384 | tf_op jit(solution)/shard_map/psum | solution.py:17
  117.9 2.5 slice_divide_fusion
  120.5 2.5 slice_divide_fusion.1
  123.2 1.1 multiply_convert_fusion.2
  136.1 2.1 add_add_fusion
  138.2 4.2 %add.732 = f32[32,8,9,256]{3,2,1,0:T(8,128)} reshape(f32[9,256,256]{2,1,0:T(8,128)} %add_add_fusion) | data formatting | bytes 4718592 | tf_op jit(solution)/shard_map/add | solution.py:235
  142.4 4.9 %copy.29 = f32[8,32,9,256]{3,1,2,0:T(8,128)} copy(f32[8,32,9,256]{3,2,0,1:T(8,128)} %bitcast.618) | data formatting | bytes 4718592 | tf_op jit(solution)/shard_map/transpose | solution.py:23
  147.3 4.6 %all-to-all-start = ((f32[8,32,9,256]{3,1,2,0:T(8,128)}), f32[8,32,9,256]{3,1,2,0:T(8,128)}, u32[]{:S(2)}, u32[]{:S(2)}) async-start(f32[8,32,9,256]{3,1,2,0:T(8,128)} %copy.29), calls=%async_computation | async-start | bytes 4718592 | tf_op jit(solution)/shard_map/all_to_all | solution.py:28
  155.1 2.4 pad_slice_fusion.16
  157.5 1.3 reshape.1166
  158.8 1.3 reshape.1160
  161.4 1.3 reshape.1163
  162.7 1.3 reshape.1164
  167.4 1.0 convolution_add_fusion.52
  171.9 1.4 reshape.1151
  173.3 1.4 reshape.1152
  174.6 1.4 reshape.1153
  176.0 1.4 reshape.1154
  180.1 0.9 convolution_add_fusion.39
  182.8 1.0 convolution_add_fusion.36
  187.1 1.1 fusion.127
  192.5 1.9 reduce_sum.218
  194.4 1.0 copy.30
  195.4 6.2 %all-to-all-start.1 = ((f32[32,9,256]{2,1,0:T(8,128)}), f32[32,9,256]{2,1,0:T(8,128)S(1)}, u32[]{:S(2)}, u32[]{:S(2)}) async-start(f32[32,9,256]{2,1,0:T(8,128)} %copy.30), calls=%async_computation.1 | async-start | bytes 1048576 | tf_op jit(solution)/shard_map/all_to_all | solution.py:35
  201.7 1.4 pad_slice_fusion
  203.9 14.4 %all-to-all-done.1 = f32[32,9,256]{2,1,0:T(8,128)S(1)} async-done(((f32[32,9,256]{2,1,0:T(8,128)}), f32[32,9,256]{2,1,0:T(8,128)S(1)}, u32[]{:S(2)}, u32[]{:S(2)}) %all-to-all-start.1) | async-done | bytes 294944 | tf_op jit(solution)/shard_map/all_to_all | solution.py:35
  219.2 5.1 %all-to-all-start.2 = ((f32[32,9,256]{2,1,0:T(8,128)}), f32[32,9,256]{2,1,0:T(8,128)S(1)}, u32[]{:S(2)}, u32[]{:S(2)}) async-start(f32[32,9,256]{2,1,0:T(8,128)} %broadcast_in_dim.4), calls=%async_computation.2 | async-start | bytes 1048576 | tf_op jit(solution)/shard_map/all_to_all | solution.py:45
  225.5 14.2 %all-to-all-done.2 = f32[32,9,256]{2,1,0:T(8,128)S(1)} async-done(((f32[32,9,256]{2,1,0:T(8,128)}), f32[32,9,256]{2,1,0:T(8,128)S(1)}, u32[]{:S(2)}, u32[]{:S(2)}) %all-to-all-start.2) | async-done | bytes 294944 | tf_op jit(solution)/shard_map/all_to_all | solution.py:45
  239.9 1.7 broadcast_in_dim.5
  241.6 7.7 %all-to-all-start.3 = ((f32[8,32,9,256]{3,1,2,0:T(8,128)}), f32[8,32,9,256]{3,1,2,0:T(8,128)}, u32[]{:S(2)}, u32[]{:S(2)}) async-start(f32[8,32,9,256]{3,1,2,0:T(8,128)} %broadcast_in_dim.5), calls=%async_computation.3 | async-start | bytes 4718592 | tf_op jit(solution)/shard_map/all_to_all | solution.py:45
  253.4 1.1 multiply_convert_fusion.1
  254.4 24.0 %all-to-all-done.3 = f32[8,32,9,256]{3,1,2,0:T(8,128)} async-done(((f32[8,32,9,256]{3,1,2,0:T(8,128)}), f32[8,32,9,256]{3,1,2,0:T(8,128)}, u32[]{:S(2)}, u32[]{:S(2)}) %all-to-all-start.3) | async-done | bytes 2359328 | tf_op jit(solution)/shard_map/all_to_all | solution.py:45
  278.4 1.9 multiply_bitcast_fusion
  280.3 3.5 %copy.32 = f32[32,8,9,256]{3,2,1,0:T(8,128)} copy(f32[32,8,9,256]{3,0,2,1:T(8,128)S(1)} %multiply_bitcast_fusion) | data formatting | bytes 4718592 | tf_op jit(solution)/shard_map/div | solution.py:250
  283.8 4.5 %div.448 = f32[3,3,256,256]{3,2,1,0:T(8,128)} reshape(f32[32,8,9,256]{3,2,1,0:T(8,128)} %copy.32) | data formatting | bytes 4718592 | tf_op jit(solution)/shard_map/div | solution.py:250
  (504 shorter events, 66.8 us)
Async XLA Ops:
  0.6 12.1 %copy-start = (bf16[3,3,256,256]{3,2,1,0:T(8,128)(2,1)S(1)}, bf16[3,3,256,256]{3,2,1,0:T(8,128)(2,1)}, u32[]{:S(2)}) copy-start(bf16[3,3,256,256]{3,2,1,0:T(8,128)(2,1)} %param.21) | copy-start | bytes 3538948
  0.7 14.8 %copy-start.12 = (bf16[1,12,12,256]{3,2,1,0:T(8,128)(2,1)S(1)}, bf16[1,12,12,256]{3,2,1,0:T(8,128)(2,1)}, u32[]{:S(2)}) copy-start(bf16[1,12,12,256]{3,2,1,0:T(8,128)(2,1)} %param.14) | copy-start | bytes 221188
  4.3 125.0 %copy-start.34 = (f32[6,6]{1,0:T(8,128)}, f32[6,6]{1,0:T(8,128)S(1)}, u32[]{:S(2)}) copy-start(f32[6,6]{1,0:T(8,128)S(1)} %get-tuple-element.156) | copy-start | bytes 436
  7.4 118.2 %copy-start.19 = (f32[24,24]{1,0:T(8,128)}, f32[24,24]{1,0:T(8,128)S(1)}, u32[]{:S(2)}) copy-start(f32[24,24]{1,0:T(8,128)S(1)} %get-tuple-element.160) | copy-start | bytes 6916
  8.2 7.9 %copy-start.27 = (bf16[6,6,256]{2,1,0:T(8,128)(2,1)}, bf16[6,6,256]{2,1,0:T(8,128)(2,1)S(1)}, u32[]{:S(2)}) copy-start(bf16[6,6,256]{2,1,0:T(8,128)(2,1)S(1)} %bitcast_multiply_fusion.6) | copy-start | bytes 55300
  9.1 7.0 %copy-start.29 = (bf16[1,6,6,256]{3,2,1,0:T(8,128)(2,1)}, bf16[1,6,6,256]{3,2,1,0:T(8,128)(2,1)S(1)}, u32[]{:S(2)}) copy-start(bf16[1,6,6,256]{3,2,1,0:T(8,128)(2,1)S(1)} %broadcast_multiply_fusion.2) | copy-start | bytes 55300
  15.5 69.0 %copy-start.25 = (f32[3,3,256]{2,1,0:T(4,128)}, f32[3,3,256]{2,1,0:T(4,128)S(1)}, u32[]{:S(2)}) copy-start(f32[3,3,256]{2,1,0:T(4,128)S(1)} %reshape.1131) | copy-start | bytes 27652
  23.9 59.9 %copy-start.43 = (f32[1,256]{1,0:T(1,128)}, f32[1,256]{1,0:T(1,128)S(1)}, u32[]{:S(2)}) copy-start(f32[1,256]{1,0:T(1,128)S(1)} %get-tuple-element.128) | copy-start | bytes 3076
  23.9 60.3 %copy-start.64 = (f32[1,256]{1,0:T(1,128)}, f32[1,256]{1,0:T(1,128)S(1)}, u32[]{:S(2)}) copy-start(f32[1,256]{1,0:T(1,128)S(1)} %get-tuple-element.127) | copy-start | bytes 3076
  23.9 60.5 %copy-start.68 = (f32[1,256]{1,0:T(1,128)}, f32[1,256]{1,0:T(1,128)S(1)}, u32[]{:S(2)}) copy-start(f32[1,256]{1,0:T(1,128)S(1)} %get-tuple-element.129) | copy-start | bytes 3076
  23.9 60.6 %copy-start.102 = (f32[1,256]{1,0:T(1,128)}, f32[1,256]{1,0:T(1,128)S(1)}, u32[]{:S(2)}) copy-start(f32[1,256]{1,0:T(1,128)S(1)} %get-tuple-element.126) | copy-start | bytes 3076
  24.0 59.9 %copy-start.54 = (f32[1,256]{1,0:T(1,128)}, f32[1,256]{1,0:T(1,128)S(1)}, u32[]{:S(2)}) copy-start(f32[1,256]{1,0:T(1,128)S(1)} %get-tuple-element.140) | copy-start | bytes 3076
  24.0 60.2 %copy-start.86 = (f32[1,256]{1,0:T(1,128)}, f32[1,256]{1,0:T(1,128)S(1)}, u32[]{:S(2)}) copy-start(f32[1,256]{1,0:T(1,128)S(1)} %get-tuple-element.139) | copy-start | bytes 3076
  24.0 60.4 %copy-start.90 = (f32[1,256]{1,0:T(1,128)}, f32[1,256]{1,0:T(1,128)S(1)}, u32[]{:S(2)}) copy-start(f32[1,256]{1,0:T(1,128)S(1)} %get-tuple-element.141) | copy-start | bytes 3076
  24.0 60.6 %copy-start.105 = (f32[1,256]{1,0:T(1,128)}, f32[1,256]{1,0:T(1,128)S(1)}, u32[]{:S(2)}) copy-start(f32[1,256]{1,0:T(1,128)S(1)} %get-tuple-element.138) | copy-start | bytes 3076
  26.2 57.6 %copy-start.1 = (bf16[1,24,24,256]{3,2,1,0:T(8,128)(2,1)S(1)}, bf16[1,24,24,256]{3,2,1,0:T(8,128)(2,1)}, u32[]{:S(2)}) copy-start(bf16[1,24,24,256]{3,2,1,0:T(8,128)(2,1)} %param.17) | copy-start | bytes 884740
  26.8 57.4 %copy-start.10 = (bf16[1,12,12,256]{3,2,1,0:T(8,128)(2,1)S(1)}, bf16[1,12,12,256]{3,2,1,0:T(8,128)(2,1)}, u32[]{:S(2)}) copy-start(bf16[1,12,12,256]{3,2,1,0:T(8,128)(2,1)} %param.18) | copy-start | bytes 221188
  26.8 57.6 %copy-start.18 = (bf16[1,6,6,256]{3,2,1,0:T(8,128)(2,1)S(1)}, bf16[1,6,6,256]{3,2,1,0:T(8,128)(2,1)}, u32[]{:S(2)}) copy-start(bf16[1,6,6,256]{3,2,1,0:T(8,128)(2,1)} %param.19) | copy-start | bytes 55300
  27.1 57.4 %copy-start.46 = (f32[3,3]{1,0:T(4,128)S(1)}, f32[3,3]{1,0:T(4,128)}, u32[]{:S(2)}) copy-start(f32[3,3]{1,0:T(4,128)} %get-tuple-element.154) | copy-start | bytes 112
  27.2 57.4 %copy-start.75 = (bf16[1,3,3,256]{3,2,1,0:T(4,128)(2,1)S(1)}, bf16[1,3,3,256]{3,2,1,0:T(4,128)(2,1)}, u32[]{:S(2)}) copy-start(bf16[1,3,3,256]{3,2,1,0:T(4,128)(2,1)} %param.20) | copy-start | bytes 13828
  81.5 41.7 %copy-start.40 = (f32[1,256]{1,0:T(1,128)}, f32[1,256]{1,0:T(1,128)S(1)}, u32[]{:S(2)}) copy-start(f32[1,256]{1,0:T(1,128)S(1)} %get-tuple-element.133) | copy-start | bytes 3076
  81.5 41.7 %copy-start.57 = (f32[1,256]{1,0:T(1,128)}, f32[1,256]{1,0:T(1,128)S(1)}, u32[]{:S(2)}) copy-start(f32[1,256]{1,0:T(1,128)S(1)} %get-tuple-element.132) | copy-start | bytes 3076
  81.5 41.7 %copy-start.61 = (f32[1,256]{1,0:T(1,128)}, f32[1,256]{1,0:T(1,128)S(1)}, u32[]{:S(2)}) copy-start(f32[1,256]{1,0:T(1,128)S(1)} %get-tuple-element.131) | copy-start | bytes 3076
  81.5 41.7 %copy-start.71 = (f32[1,256]{1,0:T(1,128)}, f32[1,256]{1,0:T(1,128)S(1)}, u32[]{:S(2)}) copy-start(f32[1,256]{1,0:T(1,128)S(1)} %get-tuple-element.130) | copy-start | bytes 3076
  82.1 41.1 %copy-start.83 = (f32[256]{0:T(256)}, f32[256]{0:T(256)S(1)}, u32[]{:S(2)}) copy-start(f32[256]{0:T(256)S(1)} %get-tuple-element.147) | copy-start | bytes 3076
  82.7 40.5 %copy-start.94 = (f32[256]{0:T(256)}, f32[256]{0:T(256)S(1)}, u32[]{:S(2)}) copy-start(f32[256]{0:T(256)S(1)} %get-tuple-element.145) | copy-start | bytes 3076
  83.3 39.9 %copy-start.79 = (f32[256]{0:T(256)}, f32[256]{0:T(256)S(1)}, u32[]{:S(2)}) copy-start(f32[256]{0:T(256)S(1)} %get-tuple-element.149) | copy-start | bytes 3076
  83.8 39.4 %copy-start.51 = (f32[256]{0:T(256)}, f32[256]{0:T(256)S(1)}, u32[]{:S(2)}) copy-start(f32[256]{0:T(256)S(1)} %get-tuple-element.151) | copy-start | bytes 3076
  117.9 5.3 %copy-start.98 = (f32[4,256]{1,0:T(4,128)}, f32[4,256]{1,0:T(4,128)S(1)}, u32[]{:S(2)}) copy-start(f32[4,256]{1,0:T(4,128)S(1)} %get-tuple-element.43) | copy-start | bytes 12292
  117.9 5.3 %copy-start.100 = (f32[4,256]{1,0:T(4,128)}, f32[4,256]{1,0:T(4,128)S(1)}, u32[]{:S(2)}) copy-start(f32[4,256]{1,0:T(4,128)S(1)} %get-tuple-element.42) | copy-start | bytes 12292
  120.5 5.1 %copy-start.110 = (f32[1,256]{1,0:T(1,128)}, f32[1,256]{1,0:T(1,128)S(1)}, u32[]{:S(2)}) copy-start(f32[1,256]{1,0:T(1,128)S(1)} %get-tuple-element.123) | copy-start | bytes 3076
  120.5 8.8 %copy-start.121 = (f32[1,256]{1,0:T(1,128)}, f32[1,256]{1,0:T(1,128)S(1)}, u32[]{:S(2)}) copy-start(f32[1,256]{1,0:T(1,128)S(1)} %get-tuple-element.121) | copy-start | bytes 3076
  120.5 11.4 %copy-start.128 = (f32[1,256]{1,0:T(1,128)}, f32[1,256]{1,0:T(1,128)S(1)}, u32[]{:S(2)}) copy-start(f32[1,256]{1,0:T(1,128)S(1)} %get-tuple-element.120) | copy-start | bytes 3076
  120.5 13.8 %copy-start.117 = (f32[1,256]{1,0:T(1,128)}, f32[1,256]{1,0:T(1,128)S(1)}, u32[]{:S(2)}) copy-start(f32[1,256]{1,0:T(1,128)S(1)} %get-tuple-element.122) | copy-start | bytes 3076
  123.1 6.2 %copy-start.122 = (f32[1,256]{1,0:T(1,128)}, f32[1,256]{1,0:T(1,128)S(1)}, u32[]{:S(2)}) copy-start(f32[1,256]{1,0:T(1,128)S(1)} %get-tuple-element.117) | copy-start | bytes 3076
  123.1 8.8 %copy-start.129 = (f32[1,256]{1,0:T(1,128)}, f32[1,256]{1,0:T(1,128)S(1)}, u32[]{:S(2)}) copy-start(f32[1,256]{1,0:T(1,128)S(1)} %get-tuple-element.116) | copy-start | bytes 3076
  123.1 11.3 %copy-start.119 = (f32[1,256]{1,0:T(1,128)}, f32[1,256]{1,0:T(1,128)S(1)}, u32[]{:S(2)}) copy-start(f32[1,256]{1,0:T(1,128)S(1)} %get-tuple-element.118) | copy-start | bytes 3076
  147.3 45.2 %all-to-all-start = ((f32[8,32,9,256]{3,1,2,0:T(8,128)}), f32[8,32,9,256]{3,1,2,0:T(8,128)}, u32[]{:S(2)}, u32[]{:S(2)}) async-start(f32[8,32,9,256]{3,1,2,0:T(8,128)} %copy.29), calls=%async_computation | async-start | bytes 4718592 | tf_op jit(solution)/shard_map/all_to_all | solution.py:28
  151.9 15.5 %copy-start.73 = (f32[1,256]{1,0:T(1,128)S(1)}, f32[1,256]{1,0:T(1,128)}, u32[]{:S(2)}) copy-start(f32[1,256]{1,0:T(1,128)} %copy-done.71) | copy-start | bytes 3076
  151.9 15.5 %copy-start.96 = (f32[256]{0:T(256)S(1)}, f32[256]{0:T(256)}, u32[]{:S(2)}) copy-start(f32[256]{0:T(256)} %copy-done.94) | copy-start | bytes 3076
  179.2 5.1 %copy-start.31 = (bf16[36,256]{1,0:T(8,128)(2,1)S(1)}, bf16[36,256]{1,0:T(8,128)(2,1)}, u32[]{:S(2)}) copy-start(bf16[36,256]{1,0:T(8,128)(2,1)} %reshape.1156) | copy-start | bytes 55300
  195.4 22.9 %all-to-all-start.1 = ((f32[32,9,256]{2,1,0:T(8,128)}), f32[32,9,256]{2,1,0:T(8,128)S(1)}, u32[]{:S(2)}, u32[]{:S(2)}) async-start(f32[32,9,256]{2,1,0:T(8,128)} %copy.30), calls=%async_computation.1 | async-start | bytes 1048576 | tf_op jit(solution)/shard_map/all_to_all | solution.py:35
  203.8 20.4 %copy-start.101 = (f32[4,256]{1,0:T(4,128)S(1)}, f32[4,256]{1,0:T(4,128)}, u32[]{:S(2)}) copy-start(f32[4,256]{1,0:T(4,128)} %copy-done.100) | copy-start | bytes 12292
  203.9 21.0 %copy-start.9 = (bf16[24,24,256]{2,1,0:T(8,128)(2,1)S(1)}, bf16[24,24,256]{2,1,0:T(8,128)(2,1)}, u32[]{:S(2)}) copy-start(bf16[24,24,256]{2,1,0:T(8,128)(2,1)} %get-tuple-element.49) | copy-start | bytes 884740
  219.2 20.5 %all-to-all-start.2 = ((f32[32,9,256]{2,1,0:T(8,128)}), f32[32,9,256]{2,1,0:T(8,128)S(1)}, u32[]{:S(2)}, u32[]{:S(2)}) async-start(f32[32,9,256]{2,1,0:T(8,128)} %broadcast_in_dim.4), calls=%async_computation.2 | async-start | bytes 1048576 | tf_op jit(solution)/shard_map/all_to_all | solution.py:45
  241.6 7.7 %copy-start.99 = (f32[4,256]{1,0:T(4,128)S(1)}, f32[4,256]{1,0:T(4,128)}, u32[]{:S(2)}) copy-start(f32[4,256]{1,0:T(4,128)} %copy-done.98) | copy-start | bytes 12292
  241.6 8.3 %copy-start.7 = (bf16[24,24,256]{2,1,0:T(8,128)(2,1)S(1)}, bf16[24,24,256]{2,1,0:T(8,128)(2,1)}, u32[]{:S(2)}) copy-start(bf16[24,24,256]{2,1,0:T(8,128)(2,1)} %get-tuple-element.51) | copy-start | bytes 884740
  241.6 36.9 %all-to-all-start.3 = ((f32[8,32,9,256]{3,1,2,0:T(8,128)}), f32[8,32,9,256]{3,1,2,0:T(8,128)}, u32[]{:S(2)}, u32[]{:S(2)}) async-start(f32[8,32,9,256]{3,1,2,0:T(8,128)} %broadcast_in_dim.5), calls=%async_computation.3 | async-start | bytes 4718592 | tf_op jit(solution)/shard_map/all_to_all | solution.py:45
  (89 other events, 168.9 us)
where the time goes:
time: 291 us; the launch traced here: 288 us
  blocking collectives  78.5 us (27%)
  local copies, waits for them, and re-layouts  55.1 us (19%)
  waiting for transfers between devices  52.6 us (18%)
  other arithmetic  38.2 us (13%)
  matrix products  35.6 us (12%)
  starting transfers between devices  23.6 us (8%)
  between operations  4.78 us (2%)
    psum x8, blocking collectives, by_axis(): value = lax.psum(value, axis)  78.5 us
    all_to_all x2, waiting for transfers between devices, from_everyone(): lax.all_to_all(jnp.broadcast_to(value[None], (peers, *value.shape)), axis...  38.2 us
    reshape x24, local copies, waits for them, and re-layouts, input_grad_rows(): window.reshape(row_count * extent, -1)  17.6 us
    dot_general x36, matrix products, input_grad_rows(): lax.dot_general(window.reshape(row_count * extent, -1), conv_weight[tap_r...  15.7 us
    all_to_all x1, waiting for transfers between devices, sum_by_axis(): return jnp.sum(lax.all_to_all(own, far, 0, 0, tiled=True), axis=0)  14.4 us
    all_to_all x2, starting transfers between devices, from_everyone(): lax.all_to_all(jnp.broadcast_to(value[None], (peers, *value.shape)), axis...  12.8 us
    dot_general x36, matrix products, conv_rows(): jnp.dot(window.reshape(row_count * extent, -1), conv_weight[tap_row, tap_...  10.4 us
    dot_general x36, matrix products, weight_grad_rows(): lax.dot_general(window.reshape(row_count * extent, -1), flat_back, (((0,)...  9.48 us
  transfers between devices with their start and end apart: 4, of which 3 were waited for; matrix products, arithmetic and copies ran while one was open for 16% of the time, Pallas kernels for 0%

commit v1 on v0

v1 whole, which is shorter than its diff:
```python
import jax
import jax.numpy as jnp
from jax import lax
from jax.experimental import pallas as pl
from jax.experimental.pallas import tpu as pltpu
from jax.sharding import Mesh
from jax.sharding import PartitionSpec as P

AXES = ("wide_0", "wide_1", "group_0", "group_1")
NZ, NX, NY, NC = 8, 4, 4, 2
MESH_ID = pl.DeviceIdType.MESH
EPSILON = 1e-05
F32 = jnp.float32
BF16 = jnp.bfloat16

ROWS, COLS = 40, 32
PLACES = ((1, 0, 24), (26, 0, 12), (26, 16, 6), (26, 24, 3))
UP = (1, 25)
LOW = (26, 38)

CHUNKS = ((0, 2, 0), (2, 2, 1), (4, 2, 0), (6, 3, 1))


def kernel(
    f4, f5, f6, f7, g4, g5, g6, g7, w_hbm, gain_ref, shift_ref, h_ref, wd_ref,
    o4, o5, o6, o7, d4, d5, d6, d7, dw_hbm, dg_ref, ds_ref,
    vf4, vf5, vf6, vf7, vg4, vg5, vg6, vg7, w, wt,
    fc, gc, mask, x3, xt, conv, norm, slope, b3, res,
    sb, s0r, s1, s2,
    dw, d2r, acc1, r1, acc2, r2, acc3, zr, final,
    in_sem, st_s, st_r, c_s, c_r, out_sem,
):
    z = lax.axis_index("wide_0")
    x = lax.axis_index("wide_1")
    y = lax.axis_index("group_0")
    c = lax.axis_index("group_1")
    other = 1 - c

    barrier = pltpu.get_barrier_semaphore()

    def greet(dev):
        pl.semaphore_signal(barrier, inc=1, device_id=dev, device_id_type=MESH_ID)

    greet((z, x, y, other))
    for dx in range(NX):
        for dy in range(NY):
            if dx or dy:
                greet((z, (x + dx) % NX, (y + dy) % NY, c))
    for dz in range(1, NZ):
        for dc in range(NC):
            greet(((z + dz) % NZ, x, y, (c + dc) % NC))

    loads = []
    for i, (src, dst) in enumerate(
        ((f4, vf4), (f5, vf5), (f6, vf6), (f7, vf7), (w_hbm, w),
         (g4, vg4), (g5, vg5), (g6, vg6), (g7, vg7))
    ):
        copy = pltpu.make_async_copy(src, dst, in_sem.at[i])
        copy.start()
        loads.append(copy)

    def rows_at(r):
        return pl.ds(pl.multiple_of(r * COLS, COLS), COLS)

    limits = []
    for k in range(4):
        stride = 16 * 2**k
        limits.append(((h_ref[0] + stride - 1) // stride, (wd_ref[0] + stride - 1) // stride))
    col = lax.broadcasted_iota(jnp.int32, (COLS, 256), 0)

    def clear_row(r, carry):
        fc[r] = jnp.zeros((COLS, 256), F32)
        gc[r] = jnp.zeros((COLS, 256), F32)
        mask[rows_at(r)] = jnp.zeros((COLS, 256), F32)
        return carry

    lax.fori_loop(0, ROWS, clear_row, 0)

    def clear_b3(r, carry):
        b3[rows_at(r)] = jnp.zeros((COLS, 768), BF16)
        return carry

    lax.fori_loop(0, ROWS + 2, clear_b3, 0)

    def mask_up(r, carry):
        inside = jnp.logical_and(
            r - UP[0] < jnp.minimum(limits[0][0], 24), col < jnp.minimum(limits[0][1], 24)
        )
        mask[rows_at(r)] = jnp.where(inside, 1.0, 0.0)
        return carry

    lax.fori_loop(UP[0], UP[1], mask_up, 0)

    def mask_low(r, carry):
        inside = None
        for k in (1, 2, 3):
            _, first, side = PLACES[k]
            here = jnp.logical_and(
                r - LOW[0] < jnp.minimum(limits[k][0], side),
                jnp.logical_and(
                    col >= first, col - first < jnp.minimum(limits[k][1], side)
                ),
            )
            inside = here if inside is None else jnp.logical_or(inside, here)
        mask[rows_at(r)] = jnp.where(inside, 1.0, 0.0)
        return carry

    lax.fori_loop(LOW[0], LOW[1], mask_low, 0)

    for k, ref in enumerate((vf4, vf5, vf6, vf7)):
        loads[k].wait()
        first_row, first, side = PLACES[k]
        fc[first_row : first_row + side, first : first + side, :] = ref[0].astype(F32)

    def spread(r, carry):
        value = fc[r] * mask[rows_at(r)]
        at = rows_at(r)
        x3[at, 0:256] = pltpu.roll(value, 1, 0).astype(BF16)
        x3[at, 256:512] = value.astype(BF16)
        x3[at, 512:768] = pltpu.roll(value, COLS - 1, 0).astype(BF16)
        return carry

    lax.fori_loop(0, ROWS, spread, 0)
    loads[4].wait()

    flat = (LOW[1] - 1) * COLS
    total = None
    for a in range(3):
        part = jnp.dot(
            x3[a * COLS : a * COLS + flat, :],
            w[a * 768 : (a + 1) * 768, :],
            preferred_element_type=F32,
        )
        total = part if total is None else total + part
    conv[COLS : COLS + flat, :] = total

    zero = jnp.zeros((COLS, 256), F32)

    def down(value):
        return jnp.sum(value, axis=0, keepdims=True)

    def by_level(up, low):
        out = [down(up)]
        for k in (1, 2, 3):
            _, first, side = PLACES[k]
            out.append(down(jnp.where(jnp.logical_and(col >= first, col < first + 8 * (1 if k > 1 else 2)), low, 0.0)))
        return out

    def moments(r, carry):
        s, q, n = carry
        m = mask[rows_at(r)]
        v = conv[rows_at(r)]
        mv = m * v
        return s + mv, q + mv * v, n + m

    up = lax.fori_loop(UP[0], UP[1], moments, (zero, zero, zero))
    low = lax.fori_loop(LOW[0], LOW[1], moments, (zero, zero, zero))
    sums = by_level(up[0], low[0])
    squares = by_level(up[1], low[1])
    tallies = by_level(up[2], low[2])
    lane = lax.broadcasted_iota(jnp.int32, (1, 256), 1)
    counts_row = jnp.zeros((1, 256), F32)
    for k in range(4):
        counts_row = jnp.where(lane // 64 == k, tallies[k], counts_row)

    def remote(src, dst, send, recv, dev):
        return pltpu.make_async_remote_copy(
            src_ref=src, dst_ref=dst, send_sem=send, recv_sem=recv,
            device_id=dev, device_id_type=MESH_ID,
        )

    pl.semaphore_wait(barrier, 30)

    def stats(which, halves, filler_a=None, filler_b=None):
        for half in range(2):
            for i, row in enumerate(halves[half]):
                sb[which, half, i] = row
        first = remote(
            sb.at[which, other], s0r.at[which], st_s.at[which, 0], st_r.at[which, 0],
            (z, x, y, other),
        )
        first.start()
        first.wait()
        own = x * NY + y
        s1[which, own] = sb[which, c] + s0r[which]
        plane = []
        for dx in range(NX):
            for dy in range(NY):
                if dx or dy:
                    slot = 1 + dx * NY + dy
                    plane.append(remote(
                        s1.at[which, own], s1.at[which, own],
                        st_s.at[which, slot], st_r.at[which, slot],
                        (z, (x + dx) % NX, (y + dy) % NY, c),
                    ))
        for copy in plane:
            copy.start()
        if filler_a is not None:
            filler_a()
        for copy in plane:
            copy.wait()
        value = s1[which, 0]
        for i in range(1, NX * NY):
            value = value + s1[which, i]
        s2[which, c, z] = value
        column = []
        for dz in range(NZ):
            for dc in range(NC):
                if dz or dc:
                    slot = 17 + dz * NC + dc
                    column.append(remote(
                        s2.at[which, c, z], s2.at[which, c, z],
                        st_s.at[which, slot], st_r.at[which, slot],
                        ((z + dz) % NZ, x, y, (c + dc) % NC),
                    ))
        for copy in column:
            copy.start()
        if filler_b is not None:
            filler_b()
        for copy in column:
            copy.wait()
        outs = []
        for half in range(2):
            value = s2[which, half, 0]
            for i in range(1, NZ):
                value = value + s2[which, half, i]
            outs.append([value[i] for i in range(5)])
        return outs

    def fill_transposes():
        def turn(b, carry):
            at = pl.ds(pl.multiple_of(b * 256, 256), 256)
            xt[at, :] = x3[:, at].T
            return carry

        for b in range(3):
            xt[b * 256 : (b + 1) * 256, :] = x3[:, b * 256 : (b + 1) * 256].T

    def fill_weights():
        def turn(t, carry):
            at = pl.ds(pl.multiple_of(t * 256, 256), 256)
            wt[at, :] = w[at, :].T
            return carry

        lax.fori_loop(0, 9, turn, 0)
        for k, ref in enumerate((vg4, vg5, vg6, vg7)):
            loads[5 + k].wait()
            first_row, first, side = PLACES[k]
            gc[first_row : first_row + side, first : first + side, :] = ref[0].astype(F32)

    (sum_rows, square_rows) = stats(
        0, (sums + [counts_row], squares + [counts_row]), fill_transposes, fill_weights
    )
    means, inverses, counts = [], [], []
    for k in range(4):
        n = down(jnp.where(lane == 64 * k, sum_rows[4], 0.0).T).T if False else jnp.sum(
            jnp.where(lane == 64 * k, sum_rows[4], 0.0), axis=1, keepdims=True
        )
        n = jnp.broadcast_to(n, (1, 256))
        mean = sum_rows[k] / n
        counts.append(n)
        means.append(mean)
        inverses.append(lax.rsqrt(square_rows[k] / n - mean * mean + EPSILON))
    gains = [gain_ref[k : k + 1, :] for k in range(4)]
    shifts = [shift_ref[k : k + 1, :] for k in range(4)]

    def low_of(rows):
        return jnp.where(col < 16, rows[1], jnp.where(col < 24, rows[2], rows[3]))

    def activate(params):
        mean, inverse, gain, shift = params

        def step(r, carry):
            s, g = carry
            at = rows_at(r)
            m = mask[at]
            normed = (conv[at] - mean) * inverse
            shifted = gain * normed + shift
            sig = jax.nn.sigmoid(shifted)
            res[r] = m * shifted * sig
            slope_value = m * gc[r] * sig * (1.0 + shifted * (1.0 - sig))
            norm[at] = normed
            slope[at] = slope_value
            return s + slope_value, g + slope_value * normed

        return step

    up_params = (means[0], inverses[0], gains[0], shifts[0])
    low_params = (low_of(means), low_of(inverses), low_of(gains), low_of(shifts))
    up = lax.fori_loop(UP[0], UP[1], activate(up_params), (zero, zero))
    low = lax.fori_loop(LOW[0], LOW[1], activate(low_params), (zero, zero))
    shift_local = by_level(up[0], low[0])
    gain_local = by_level(up[1], low[1])

    def take_out(refs):
        for k, ref in enumerate(refs):
            first_row, first, side = PLACES[k]
            ref[0] = res[first_row : first_row + side, first : first + side, :].astype(BF16)

    (shift_rows, gain_rows) = stats(
        1, (shift_local + [counts_row], gain_local + [counts_row]),
        lambda: take_out((o4, o5, o6, o7)),
    )
    for k in range(4):
        dg_ref[k : k + 1, :] = gain_rows[k] * (1.0 / 256.0)
        ds_ref[k : k + 1, :] = shift_rows[k] * (1.0 / 256.0)

    def back(params):
        scale, base, lean = params

        def step(r, carry):
            at = rows_at(r)
            value = mask[at] * scale * (slope[at] - base - norm[at] * lean)
            value = value.astype(BF16).astype(F32)
            to = rows_at(r + 1)
            b3[to, 0:256] = pltpu.roll(value, COLS - 1, 0).astype(BF16)
            b3[to, 256:512] = value.astype(BF16)
            b3[to, 512:768] = pltpu.roll(value, 1, 0).astype(BF16)
            return carry

        return step

    scales = [gains[k] * inverses[k] for k in range(4)]
    bases = [shift_rows[k] / counts[k] for k in range(4)]
    leans = [gain_rows[k] / counts[k] for k in range(4)]
    lax.fori_loop(UP[0], UP[1], back((scales[0], bases[0], leans[0])), 0)
    lax.fori_loop(LOW[0], LOW[1], back((low_of(scales), low_of(bases), low_of(leans))), 0)

    def ring(axis, d):
        if axis == 0:
            return (z, (x + d) % NX, y, c)
        return (z, x, (y + d) % NY, c)

    def place(axis):
        return x if axis == 0 else y

    def shifted_place(axis, d):
        return (place(axis) + d) % 4

    def al(value, unit):
        return pl.multiple_of(value, unit)

    pending = {}

    def start(key, copies):
        for copy in copies:
            copy.start()
        pending[key] = copies

    def finish(key):
        for copy in pending.pop(key):
            copy.wait()

    def sems(i, slot):
        return c_s.at[i, slot], c_r.at[i, slot]

    def stage0(i):
        t0, nt, axis = CHUNKS[i]
        for t in range(t0, t0 + nt):
            a, b = divmod(t, 3)
            dw[t] = jnp.dot(
                xt[b * 256 : (b + 1) * 256, :],
                b3[(2 - a) * COLS : (2 - a) * COLS + ROWS * COLS, 256:512],
                preferred_element_type=F32,
            )
        start((0, i), [remote(
            dw.at[pl.ds(t0, nt), pl.ds(al(other * 128, 128), 128), :],
            d2r.at[pl.ds(t0, nt)], *sems(i, 0), (z, x, y, other),
        )])

    def stage1(i):
        t0, nt, axis = CHUNKS[i]
        finish((0, i))
        for t in range(t0, t0 + nt):
            acc1[t] = dw[t, pl.ds(al(c * 128, 128), 128), :] + d2r[t]
        start((1, i), [remote(
            acc1.at[pl.ds(t0, nt), pl.ds(al(shifted_place(axis, d) * 32, 32), 32), :],
            r1.at[d - 1, pl.ds(t0, nt)], *sems(i, d), ring(axis, d),
        ) for d in (1, 2, 3)])

    def stage2(i):
        t0, nt, axis = CHUNKS[i]
        second = 1 - axis
        finish((1, i))
        for t in range(t0, t0 + nt):
            own = acc1[t, pl.ds(al(place(axis) * 32, 32), 32), :]
            acc2[t] = own + r1[0, t] + r1[1, t] + r1[2, t]
        start((2, i), [remote(
            acc2.at[pl.ds(t0, nt), pl.ds(al(shifted_place(second, d) * 8, 8), 8), :],
            r2.at[d - 1, pl.ds(t0, nt)], *sems(i, 3 + d), ring(second, d),
        ) for d in (1, 2, 3)])

    def stage3(i):
        t0, nt, axis = CHUNKS[i]
        second = 1 - axis
        finish((2, i))
        for t in range(t0, t0 + nt):
            own = acc2[t, pl.ds(al(place(second) * 8, 8), 8), :]
            acc3[t] = own + r2[0, t] + r2[1, t] + r2[2, t]
        start((3, i), [remote(
            acc3.at[pl.ds(t0, nt), pl.ds((z + d) % NZ, 1), :],
            zr.at[pl.ds(t0, nt), pl.ds(z, 1), :], *sems(i, 6 + d), ((z + d) % NZ, x, y, c),
        ) for d in range(1, NZ)])
        for t in range(t0, t0 + nt):
            zr[t, pl.ds(z, 1), :] = acc3[t, pl.ds(z, 1), :]

    def home(axis):
        return c * 128 + place(axis) * 32

    def stage4(i):
        t0, nt, axis = CHUNKS[i]
        second = 1 - axis
        finish((3, i))
        row = home(axis) + place(second) * 8 + z
        for t in range(t0, t0 + nt):
            final[t, pl.ds(row, 1), :] = jnp.sum(zr[t], axis=0, keepdims=True) * (1.0 / 256.0)
        here = final.at[pl.ds(t0, nt), pl.ds(row, 1), :]
        start((4, i), [remote(
            here, here, *sems(i, 13 + d), ((z + d) % NZ, x, y, c),
        ) for d in range(1, NZ)])

    def stage5(i):
        t0, nt, axis = CHUNKS[i]
        second = 1 - axis
        finish((4, i))
        here = final.at[pl.ds(t0, nt), pl.ds(al(home(axis) + place(second) * 8, 8), 8), :]
        start((5, i), [remote(
            here, here, *sems(i, 20 + d), ring(second, d),
        ) for d in (1, 2, 3)])

    def stage6(i):
        t0, nt, axis = CHUNKS[i]
        finish((5, i))
        here = final.at[pl.ds(t0, nt), pl.ds(al(home(axis), 32), 32), :]
        start((6, i), [remote(
            here, here, *sems(i, 23 + d), ring(axis, d),
        ) for d in (1, 2, 3)])

    def stage7(i):
        t0, nt, axis = CHUNKS[i]
        finish((6, i))
        here = final.at[pl.ds(t0, nt), pl.ds(al(c * 128, 128), 128), :]
        start((7, i), [remote(here, here, *sems(i, 27), (z, x, y, other))])

    def stage8(i):
        t0, nt, axis = CHUNKS[i]
        finish((7, i))
        copy = pltpu.make_async_copy(
            final.at[pl.ds(t0, nt)], dw_hbm.at[pl.ds(t0, nt)], out_sem.at[i]
        )
        copy.start()
        pending[(8, i)] = [copy]

    stages = (stage0, stage1, stage2, stage3, stage4, stage5, stage6, stage7, stage8)
    count = len(CHUNKS)

    for i in range(count):
        stage0(i)
        if i:
            stage1(i - 1)
    stage1(count - 1)

    total = None
    for a in range(3):
        part = jnp.dot(
            b3[(3 - a) * COLS : (3 - a) * COLS + flat, :],
            wt[a * 768 : (a + 1) * 768, :],
            preferred_element_type=F32,
        )
        total = part if total is None else total + part
    conv[COLS : COLS + flat, :] = total

    def masked(r, carry):
        res[r] = conv[rows_at(r)] * mask[rows_at(r)]
        return carry

    lax.fori_loop(1, LOW[1], masked, 0)
    take_out((d4, d5, d6, d7))

    for step in range(2, 9 + count - 1):
        for i in range(count):
            s = step - i
            if 2 <= s <= 8:
                stages[s](i)
    for i in range(count):
        finish((8, i))


def shards(*args):
    (f4, f5, f6, f7, g4, g5, g6, g7, conv_weight, gain, shift, heights, widths) = args
    any_spec = pl.BlockSpec(memory_space=pl.ANY)
    vmem_spec = pl.BlockSpec(memory_space=pltpu.VMEM)
    smem_spec = pl.BlockSpec(memory_space=pltpu.SMEM)
    feats = (f4, f5, f6, f7)
    image_shapes = [jax.ShapeDtypeStruct(f.shape, BF16) for f in feats]
    vm = pltpu.VMEM
    scratch = (
        [vm(f.shape, BF16) for f in feats]
        + [vm(f.shape, BF16) for f in feats]
        + [
            vm((2304, 256), BF16),
            vm((2304, 256), BF16),
            vm((ROWS, COLS, 256), F32),
            vm((ROWS, COLS, 256), F32),
            vm((ROWS * COLS, 256), F32),
            vm((ROWS * COLS, 768), BF16),
            vm((768, ROWS * COLS), BF16),
            vm((ROWS * COLS, 256), F32),
            vm((ROWS * COLS, 256), F32),
            vm((ROWS * COLS, 256), F32),
            vm(((ROWS + 2) * COLS, 768), BF16),
            vm((ROWS, COLS, 256), F32),
            vm((2, 2, 5, 1, 256), F32),
            vm((2, 5, 1, 256), F32),
            vm((2, 16, 5, 1, 256), F32),
            vm((2, 2, 8, 5, 1, 256), F32),
            vm((9, 256, 256), F32),
            vm((9, 128, 256), F32),
            vm((9, 128, 256), F32),
            vm((3, 9, 32, 256), F32),
            vm((9, 32, 256), F32),
            vm((3, 9, 8, 256), F32),
            vm((9, 8, 256), F32),
            vm((9, 8, 256), F32),
            vm((9, 256, 256), F32),
            pltpu.SemaphoreType.DMA((9,)),
            pltpu.SemaphoreType.DMA((2, 33)),
            pltpu.SemaphoreType.DMA((2, 33)),
            pltpu.SemaphoreType.DMA((len(CHUNKS), 28)),
            pltpu.SemaphoreType.DMA((len(CHUNKS), 28)),
            pltpu.SemaphoreType.DMA((len(CHUNKS),)),
        ]
    )
    small = jax.ShapeDtypeStruct((4, 256), F32)
    outs = pl.pallas_call(
        kernel,
        out_shape=image_shapes + image_shapes + [jax.ShapeDtypeStruct((9, 256, 256), F32), small, small],
        in_specs=[any_spec] * 9 + [vmem_spec] * 2 + [smem_spec] * 2,
        out_specs=[vmem_spec] * 8 + [any_spec] + [vmem_spec] * 2,
        scratch_shapes=scratch,
        compiler_params=pltpu.CompilerParams(
            collective_id=0, has_side_effects=True, vmem_limit_bytes=60 * 1024 * 1024
        ),
        name="fused_step",
    )(f4, f5, f6, f7, g4, g5, g6, g7, conv_weight.reshape(2304, 256), gain, shift, heights, widths)
    outs = list(outs)
    outs[8] = outs[8].reshape(3, 3, 256, 256)
    return tuple(outs)


def solution(mesh):
    torus = Mesh(mesh.devices.reshape(NZ, NX, NY, NC), AXES)
    image = P(AXES, None, None, None)
    in_specs = (image,) * 8 + (P(), P(), P(), P(AXES), P(AXES))
    out_specs = (image,) * 8 + (P(), P(), P())
    return jax.shard_map(shards, mesh=torus, in_specs=in_specs, out_specs=out_specs, check_vma=False)
```

time: 291 us -> 108 us (0.37)
  Pallas kernels: 0 us -> 89.9 us
  blocking collectives: 78.5 us -> 0 us
  waiting for transfers between devices: 52.6 us -> 0 us
  local copies, waits for them, and re-layouts: 55.1 us -> 16.2 us
  other arithmetic: 38.2 us -> 0 us
  matrix products: 35.6 us -> 0 us
  starting transfers between devices: 23.6 us -> 0 us
    pallas_call x0 -> x1, Pallas kernels: none -> 89.9 us  [shards(): pl.pallas_call(kernel, out_shape=image_shapes + image_shapes + [jax.Shape...]
    psum x8 -> x0, blocking collectives: 78.5 us -> none  [by_axis(): value = lax.psum(value, axis)]
    all_to_all x4 -> x0, waiting for transfers between devices: 52.6 us -> none  [the longest x2 38.2 us: from_everyone(): lax.all_to_all(jnp.broadcast_to(value[None], (peers, *value.shape)), axis...]
    dot_general x108 -> x0, matrix products: 35.6 us -> none  [the longest x36 15.7 us: input_grad_rows(): lax.dot_general(window.reshape(row_count * extent, -1), conv_weight[tap_r...]
    all_to_all x4 -> x0, starting transfers between devices: 23.6 us -> none  [the longest x2 12.8 us: from_everyone(): lax.all_to_all(jnp.broadcast_to(value[None], (peers, *value.shape)), axis...]
    reshape x57 -> x0, local copies, waits for them, and re-layouts: 21.2 us -> none  [the longest x24 17.6 us: input_grad_rows(): window.reshape(row_count * extent, -1)]
    div x7 -> x0, other arithmetic: 13.3 us -> none  [the longest x1 2.55 us: shards(): mean_value = moment_sums[level_index] / pixel_count]
    unnamed x266 -> x15, local copies, waits for them, and re-layouts: 3.54 us -> 16.2 us
  transfers between devices with their start and end apart: 4 -> 0, of which waited for: 3 -> 0; matrix products, arithmetic and copies ran while one was open for 16% -> 0% of each run, Pallas kernels for 0% -> 0%
where the time goes in v1:
time: 108 us
  Pallas kernels  89.9 us (83%)
  local copies, waits for them, and re-layouts  16.2 us (15%)
  between operations  1.96 us (2%)
    pallas_call x1, Pallas kernels, shards(): pl.pallas_call(kernel, out_shape=image_shapes + image_shapes + [jax.Shape...  89.9 us
    unnamed x15, local copies, waits for them, and re-layouts  16.2 us

profile of v1, /device:TPU:1, one launch (start us, length us, event | category | flops | bytes accessed | tf_op | source)
XLA Modules:
  0.0 108.0 jit_solution(889148137468418364)
XLA Ops:
  1.9 89.9 %fused_step.1 = (bf16[1,24,24,256]{3,2,1,0:T(8,128)(2,1)}, bf16[1,12,12,256]{3,2,1,0:T(8,128)(2,1)}, bf16[1,6,6,256]{3,2,1,0:T(8,128)(2,1)}, bf16[1,3,3,256]{3,2...) custom-call(bf16[1,24,24,256]{3,2,1,0:T(8,128)(2,1)} %f4.1, ...), custom_call_target="tpu_custom_call" | custom-call | tf_op jit(solution)/shard_map/fused_step/pallas_call | solution.py:535
  91.8 1.7 %copy.37 = bf16[1,24,24,256]{3,2,1,0:T(8,128)(2,1)} copy(bf16[1,24,24,256]{3,2,1,0:T(8,128)(2,1)} %get-tuple-element.44) | data formatting | bytes 589824
  93.5 1.5 %copy.38 = bf16[1,12,12,256]{3,2,1,0:T(8,128)(2,1)} copy(bf16[1,12,12,256]{3,2,1,0:T(8,128)(2,1)} %get-tuple-element.45) | data formatting | bytes 147456
  95.0 1.3 %copy.39 = bf16[1,6,6,256]{3,2,1,0:T(8,128)(2,1)} copy(bf16[1,6,6,256]{3,2,1,0:T(8,128)(2,1)} %get-tuple-element.46) | data formatting | bytes 36864
  96.4 1.3 %copy.40 = bf16[1,3,3,256]{3,2,1,0:T(4,128)(2,1)} copy(bf16[1,3,3,256]{3,2,1,0:T(4,128)(2,1)} %get-tuple-element.47) | data formatting | bytes 9216
  97.7 1.7 %copy.41 = bf16[1,24,24,256]{3,2,1,0:T(8,128)(2,1)} copy(bf16[1,24,24,256]{3,2,1,0:T(8,128)(2,1)} %get-tuple-element.48) | data formatting | bytes 589824
  99.4 1.5 %copy.42 = bf16[1,12,12,256]{3,2,1,0:T(8,128)(2,1)} copy(bf16[1,12,12,256]{3,2,1,0:T(8,128)(2,1)} %get-tuple-element.49) | data formatting | bytes 147456
  100.9 1.3 %copy.43 = bf16[1,6,6,256]{3,2,1,0:T(8,128)(2,1)} copy(bf16[1,6,6,256]{3,2,1,0:T(8,128)(2,1)} %get-tuple-element.50) | data formatting | bytes 36864
  102.3 1.3 %copy.44 = bf16[1,3,3,256]{3,2,1,0:T(4,128)(2,1)} copy(bf16[1,3,3,256]{3,2,1,0:T(4,128)(2,1)} %get-tuple-element.51) | data formatting | bytes 9216
  103.5 0.0 copy-start.1
  103.5 0.0 copy-start
  103.5 3.2 %copy.45 = f32[3,3,256,256]{3,2,1,0:T(8,128)} copy(f32[3,3,256,256]{3,2,1,0:T(8,128)} %bitcast.2) | data formatting | bytes 4718592
  106.8 0.0 copy-done.1
  106.8 0.6 copy.46
  107.4 0.0 copy-done
  107.4 0.6 copy.47
Async XLA Ops:
  103.5 3.2 %copy-start.1 = (f32[4,256]{1,0:T(4,128)S(1)}, f32[4,256]{1,0:T(4,128)}, u32[]{:S(2)}) copy-start(f32[4,256]{1,0:T(4,128)} %get-tuple-element.53) | copy-start | bytes 12292
  103.5 3.8 %copy-start = (f32[4,256]{1,0:T(4,128)S(1)}, f32[4,256]{1,0:T(4,128)}, u32[]{:S(2)}) copy-start(f32[4,256]{1,0:T(4,128)} %get-tuple-element.54) | copy-start | bytes 12292

commit v2 on v1

--- a/solution.py
+++ b/solution.py
@@ -18,17 +18,20 @@
 UP = (1, 25)
 LOW = (26, 38)
 
+FUSED_VMEM = 63_780_000
+
 CHUNKS = ((0, 2, 0), (2, 2, 1), (4, 2, 0), (6, 3, 1))
 
 
 def kernel(
-    f4, f5, f6, f7, g4, g5, g6, g7, w_hbm, gain_ref, shift_ref, h_ref, wd_ref,
-    o4, o5, o6, o7, d4, d5, d6, d7, dw_hbm, dg_ref, ds_ref,
+    f4, f5, f6, f7, g4, g5, g6, g7, w_hbm, gain_hbm, shift_hbm, size_hbm,
+    o4, o5, o6, o7, d4, d5, d6, d7, final, dg_ref, ds_ref,
+    gain_ref, shift_ref, size_ref,
     vf4, vf5, vf6, vf7, vg4, vg5, vg6, vg7, w, wt,
     fc, gc, mask, x3, xt, conv, norm, slope, b3, res,
     sb, s0r, s1, s2,
-    dw, d2r, acc1, r1, acc2, r2, acc3, zr, final,
-    in_sem, st_s, st_r, c_s, c_r, out_sem,
+    dw, d2r, acc1, r1, acc2, r2, zs, zr, zg,
+    in_sem, st_s, st_r, c_s, c_r,
 ):
     z = lax.axis_index("wide_0")
     x = lax.axis_index("wide_1")
@@ -53,7 +56,8 @@
     loads = []
     for i, (src, dst) in enumerate(
         ((f4, vf4), (f5, vf5), (f6, vf6), (f7, vf7), (w_hbm, w),
-         (g4, vg4), (g5, vg5), (g6, vg6), (g7, vg7))
+         (g4, vg4), (g5, vg5), (g6, vg6), (g7, vg7),
+         (gain_hbm, gain_ref), (shift_hbm, shift_ref), (size_hbm, size_ref))
     ):
         copy = pltpu.make_async_copy(src, dst, in_sem.at[i])
         copy.start()
@@ -62,10 +66,6 @@
     def rows_at(r):
         return pl.ds(pl.multiple_of(r * COLS, COLS), COLS)
 
-    limits = []
-    for k in range(4):
-        stride = 16 * 2**k
-        limits.append(((h_ref[0] + stride - 1) // stride, (wd_ref[0] + stride - 1) // stride))
     col = lax.broadcasted_iota(jnp.int32, (COLS, 256), 0)
 
     def clear_row(r, carry):
@@ -81,6 +81,20 @@
         return carry
 
     lax.fori_loop(0, ROWS + 2, clear_b3, 0)
+
+    loads[11].wait()
+    limits = []
+    for k in range(4):
+        stride = 16 * 2**k
+        limits.append([
+            jnp.broadcast_to(
+                lax.shift_right_arithmetic(
+                    size_ref[i : i + 1, :] + (stride - 1), jnp.full((1, 256), 4 + k, jnp.int32)
+                ),
+                (COLS, 256),
+            )
+            for i in range(2)
+        ])
 
     def mask_up(r, carry):
         inside = jnp.logical_and(
@@ -228,11 +242,6 @@
         return outs
 
     def fill_transposes():
-        def turn(b, carry):
-            at = pl.ds(pl.multiple_of(b * 256, 256), 256)
-            xt[at, :] = x3[:, at].T
-            return carry
-
         for b in range(3):
             xt[b * 256 : (b + 1) * 256, :] = x3[:, b * 256 : (b + 1) * 256].T
 
@@ -253,14 +262,14 @@
     )
     means, inverses, counts = [], [], []
     for k in range(4):
-        n = down(jnp.where(lane == 64 * k, sum_rows[4], 0.0).T).T if False else jnp.sum(
-            jnp.where(lane == 64 * k, sum_rows[4], 0.0), axis=1, keepdims=True
-        )
+        n = jnp.sum(jnp.where(lane == 64 * k, sum_rows[4], 0.0), axis=1, keepdims=True)
         n = jnp.broadcast_to(n, (1, 256))
         mean = sum_rows[k] / n
         counts.append(n)
         means.append(mean)
         inverses.append(lax.rsqrt(square_rows[k] / n - mean * mean + EPSILON))
+    loads[9].wait()
+    loads[10].wait()
     gains = [gain_ref[k : k + 1, :] for k in range(4)]
     shifts = [shift_ref[k : k + 1, :] for k in range(4)]
 
@@ -396,25 +405,26 @@
         finish((2, i))
         for t in range(t0, t0 + nt):
             own = acc2[t, pl.ds(al(place(second) * 8, 8), 8), :]
-            acc3[t] = own + r2[0, t] + r2[1, t] + r2[2, t]
+            value = own + r2[0, t] + r2[1, t] + r2[2, t]
+            for j in range(NZ):
+                zs[j, t] = value[j : j + 1, :]
         start((3, i), [remote(
-            acc3.at[pl.ds(t0, nt), pl.ds((z + d) % NZ, 1), :],
-            zr.at[pl.ds(t0, nt), pl.ds(z, 1), :], *sems(i, 6 + d), ((z + d) % NZ, x, y, c),
+            zs.at[(z + d) % NZ, pl.ds(t0, nt)], zr.at[d - 1, pl.ds(t0, nt)],
+            *sems(i, 6 + d), ((z + d) % NZ, x, y, c),
         ) for d in range(1, NZ)])
-        for t in range(t0, t0 + nt):
-            zr[t, pl.ds(z, 1), :] = acc3[t, pl.ds(z, 1), :]
 
     def home(axis):
         return c * 128 + place(axis) * 32
 
     def stage4(i):
         t0, nt, axis = CHUNKS[i]
-        second = 1 - axis
         finish((3, i))
-        row = home(axis) + place(second) * 8 + z
         for t in range(t0, t0 + nt):
-            final[t, pl.ds(row, 1), :] = jnp.sum(zr[t], axis=0, keepdims=True) * (1.0 / 256.0)
-        here = final.at[pl.ds(t0, nt), pl.ds(row, 1), :]
+            value = zs[z, t]
+            for d in range(1, NZ):
+                value = value + zr[d - 1, t]
+            zg[z, t] = value * (1.0 / 256.0)
+        here = zg.at[z, pl.ds(t0, nt)]
         start((4, i), [remote(
             here, here, *sems(i, 13 + d), ((z + d) % NZ, x, y, c),
         ) for d in range(1, NZ)])
@@ -423,6 +433,10 @@
         t0, nt, axis = CHUNKS[i]
         second = 1 - axis
         finish((4, i))
+        base = home(axis) + place(second) * 8
+        for t in range(t0, t0 + nt):
+            rows = [zg[j, t] for j in range(NZ)]
+            final[t, pl.ds(al(base, 8), 8), :] = jnp.concatenate(rows, axis=0)
         here = final.at[pl.ds(t0, nt), pl.ds(al(home(axis) + place(second) * 8, 8), 8), :]
         start((5, i), [remote(
             here, here, *sems(i, 20 + d), ring(second, d),
@@ -442,16 +456,7 @@
         here = final.at[pl.ds(t0, nt), pl.ds(al(c * 128, 128), 128), :]
         start((7, i), [remote(here, here, *sems(i, 27), (z, x, y, other))])
 
-    def stage8(i):
-        t0, nt, axis = CHUNKS[i]
-        finish((7, i))
-        copy = pltpu.make_async_copy(
-            final.at[pl.ds(t0, nt)], dw_hbm.at[pl.ds(t0, nt)], out_sem.at[i]
-        )
-        copy.start()
-        pending[(8, i)] = [copy]
-
-    stages = (stage0, stage1, stage2, stage3, stage4, stage5, stage6, stage7, stage8)
+    stages = (stage0, stage1, stage2, stage3, stage4, stage5, stage6, stage7)
     count = len(CHUNKS)
 
     for i in range(count):
@@ -477,25 +482,34 @@
     lax.fori_loop(1, LOW[1], masked, 0)
     take_out((d4, d5, d6, d7))
 
-    for step in range(2, 9 + count - 1):
+    for step in range(2, 8 + count - 1):
         for i in range(count):
             s = step - i
-            if 2 <= s <= 8:
+            if 2 <= s <= 7:
                 stages[s](i)
     for i in range(count):
-        finish((8, i))
+        finish((7, i))
+
+
+def write_out(*refs):
+    count = len(refs) // 2
+    sem = refs[-1]
+    copies = [pltpu.make_async_copy(refs[i], refs[count + i], sem.at[i]) for i in range(count)]
+    for copy in copies:
+        copy.start()
+    for copy in copies:
+        copy.wait()
 
 
 def shards(*args):
     (f4, f5, f6, f7, g4, g5, g6, g7, conv_weight, gain, shift, heights, widths) = args
-    any_spec = pl.BlockSpec(memory_space=pl.ANY)
+    hbm_spec = pl.BlockSpec(memory_space=pltpu.HBM)
     vmem_spec = pl.BlockSpec(memory_space=pltpu.VMEM)
-    smem_spec = pl.BlockSpec(memory_space=pltpu.SMEM)
     feats = (f4, f5, f6, f7)
-    image_shapes = [jax.ShapeDtypeStruct(f.shape, BF16) for f in feats]
     vm = pltpu.VMEM
     scratch = (
-        [vm(f.shape, BF16) for f in feats]
+        [vm((4, 256), F32), vm((4, 256), F32), vm((2, 256), jnp.int32)]
+        + [vm(f.shape, BF16) for f in feats]
         + [vm(f.shape, BF16) for f in feats]
         + [
             vm((2304, 256), BF16),
@@ -520,29 +534,41 @@
             vm((3, 9, 32, 256), F32),
             vm((9, 32, 256), F32),
             vm((3, 9, 8, 256), F32),
-            vm((9, 8, 256), F32),
-            vm((9, 8, 256), F32),
-            vm((9, 256, 256), F32),
-            pltpu.SemaphoreType.DMA((9,)),
+            vm((8, 9, 1, 256), F32),
+            vm((7, 9, 1, 256), F32),
+            vm((8, 9, 1, 256), F32),
+            pltpu.SemaphoreType.DMA((12,)),
             pltpu.SemaphoreType.DMA((2, 33)),
             pltpu.SemaphoreType.DMA((2, 33)),
             pltpu.SemaphoreType.DMA((len(CHUNKS), 28)),
             pltpu.SemaphoreType.DMA((len(CHUNKS), 28)),
-            pltpu.SemaphoreType.DMA((len(CHUNKS),)),
         ]
     )
-    small = jax.ShapeDtypeStruct((4, 256), F32)
+    results = [f.shape for f in feats] * 2
+    shapes = [(shape, BF16) for shape in results] + [((9, 256, 256), F32), ((4, 256), F32), ((4, 256), F32)]
     outs = pl.pallas_call(
         kernel,
-        out_shape=image_shapes + image_shapes + [jax.ShapeDtypeStruct((9, 256, 256), F32), small, small],
-        in_specs=[any_spec] * 9 + [vmem_spec] * 2 + [smem_spec] * 2,
-        out_specs=[vmem_spec] * 8 + [any_spec] + [vmem_spec] * 2,
+        out_shape=[vm(shape, dtype) for shape, dtype in shapes],
+        in_specs=[hbm_spec] * 12,
+        out_specs=[vmem_spec] * 11,
         scratch_shapes=scratch,
         compiler_params=pltpu.CompilerParams(
-            collective_id=0, has_side_effects=True, vmem_limit_bytes=60 * 1024 * 1024
+            collective_id=0, has_side_effects=True, vmem_limit_bytes=FUSED_VMEM
         ),
         name="fused_step",
-    )(f4, f5, f6, f7, g4, g5, g6, g7, conv_weight.reshape(2304, 256), gain, shift, heights, widths)
+    )(
+        f4, f5, f6, f7, g4, g5, g6, g7, conv_weight.reshape(2304, 256), gain, shift,
+        jnp.broadcast_to(jnp.stack([heights, widths]), (2, 256)),
+    )
+    outs = pl.pallas_call(
+        write_out,
+        out_shape=[jax.ShapeDtypeStruct(shape, dtype) for shape, dtype in shapes],
+        in_specs=[vmem_spec] * 11,
+        out_specs=[hbm_spec] * 11,
+        scratch_shapes=[pltpu.SemaphoreType.DMA((11,))],
+        compiler_params=pltpu.CompilerParams(vmem_limit_bytes=4 * 1024 * 1024),
+        name="write_out",
+    )(*outs)
     outs = list(outs)
     outs[8] = outs[8].reshape(3, 3, 256, 256)
     return tuple(outs)

time: 108 us -> 92.7 us (0.86)
  local copies, waits for them, and re-layouts: 16.2 us -> 0.65 us
    unnamed x15 -> x0, local copies, waits for them, and re-layouts: 16.2 us -> none
    pallas_call x1 -> x2, Pallas kernels: 89.9 us -> 89.9 us  [the longest x1 88.1 us: shards(): pl.pallas_call(kernel, out_shape=[vm(shape, dtype) for shape, dtype in sh...]
where the time goes in v2:
time: 92.7 us; the launch traced here: 92.6 us
  Pallas kernels  89.9 us (97%)
  between operations  1.94 us (2%)
    pallas_call x1, Pallas kernels, shards(): pl.pallas_call(kernel, out_shape=[vm(shape, dtype) for shape, dtype in sh...  88.1 us

profile of v2, /device:TPU:1, one launch (start us, length us, event | category | flops | bytes accessed | tf_op | source)
XLA Modules:
  0.0 92.6 jit_solution(5205050184160752814)
XLA Ops:
  1.9 0.1 add_bitcast_fusion
  2.0 0.6 broadcast_in_dim.8.size_hbm
  2.7 88.1 %fused_step.1 = (bf16[1,24,24,256]{3,2,1,0:T(8,128)(2,1)S(1)}, bf16[1,12,12,256]{3,2,1,0:T(8,128)(2,1)S(1)}, bf16[1,6,6,256]{3,2,1,0:T(8,128)(2,1)S(1)}, bf16[1,...) custom-call(bf16[1,24,24,256]{3,2,1,0:T(8,128)(2,1)} %f4.1, ...), custom_call_target="tpu_custom_call" | custom-call | tf_op jit(solution)/shard_map/fused_step/pallas_call | solution.py:549
  90.8 1.8 %write_out.1 = (bf16[1,24,24,256]{3,2,1,0:T(8,128)(2,1)}, bf16[1,12,12,256]{3,2,1,0:T(8,128)(2,1)}, bf16[1,6,6,256]{3,2,1,0:T(8,128)(2,1)}, bf16[1,3,3,256]{3,2,...) custom-call(bf16[1,24,24,256]{3,2,1,0:T(8,128)(2,1)S(1)} %get-tuple-, ...), custom_call_target="tpu_custom_call" | custom-call | tf_op jit(solution)/shard_map/write_out/pallas_call | solution.py:563
